TPU v7x, 256 devices: a whole 4x4x8 slice. The times are simulated.
256 devices in a mesh: row: 8 (over x, z_lo), col: 8 (over z_hi, core), depth: 4 (over y).
Axes of the slice: x: 4, y: 4, z: 8 (z_hi: 4, z_lo: 2; z = z_hi * 2 + z_lo), core: 2. Of those that a mesh axis runs over, the one named last changes fastest.
Arguments:
- alignment_matrix: bfloat16 [128, 768, 256], P('depth', 'col'), may hold values from -6 to 6
- twin_linear_matrix: bfloat16 [256, 64], replicated, may hold values from -0.375 to 0.375
- final_matrix: bfloat16 [1024, 128], replicated, may hold values from -2 to 2
- final_offset: float32 [128], replicated, may hold values from -3 to 3
- adjoint_incoming: bfloat16 [768, 768, 128], P('row', ('col', 'depth')), may hold values from -6 to 6
Outputs:
- contact_delta: bfloat16 [768, 768, 128], P('row', ('col', 'depth'))
- alignment_adjoint: float32 [128, 768, 256], P('depth', 'col')
- grad_w_out: float32 [1024, 128], replicated
- grad_b_out: float32 [128], replicated
All inputs are finite; a program needn't handle non-finite values.
Results may differ from a plain program's by a relative error of at most 0.007.
Values may be sent and summed in bfloat16 or wider, within the bound.
No kernel may reach another device: no remote copies, remote signals or barrier semaphores. Data moves between devices by JAX's collectives and lax.ppermute only.
A program may use at most 128 MiB of HBM per device.

v0:
```python
import jax
import jax.numpy as jnp
from jax import lax
from jax.sharding import PartitionSpec as P

epsilon = 1e-05


def in_one(arrays, axis):
    vector, at, gathered = (jnp.concatenate([a.reshape(-1) for a in arrays]), 0, [])
    running = lax.psum(vector, axis)
    for a in arrays:
        gathered.append(running[at : at + a.size].reshape(a.shape))
        at += a.size
    return tuple(gathered)


def broadcast(shard, axis, root):
    return lax.dynamic_index_in_dim(lax.all_gather(shard, axis), root, 0, keepdims=False)


def copy_for_each(shard, axis):
    copies = jnp.broadcast_to(shard, (lax.axis_size(axis), *shard.shape))
    return lax.all_to_all(copies, axis, split_axis=0, concat_axis=0, tiled=True)


def of_everyone(shard, axis):
    everything = copy_for_each(shard, axis)
    return jnp.sum(everything, axis=0)


def standardize_channels(values):
    centre = jnp.mean(values, axis=-1, keepdims=True)
    spread = jnp.mean(jnp.square(values - centre), axis=-1, keepdims=True)
    return (values - centre) * lax.rsqrt(spread + epsilon)


def body(alignment_matrix, twin_linear_matrix, final_matrix, final_offset, adjoint_incoming):
    alignment_share, amino_share, discarded_item = alignment_matrix.shape
    latent_features = twin_linear_matrix.shape[1] // 2
    row_count = lax.axis_size("row")
    col_count = lax.axis_size("col")
    depth_count = lax.axis_size("depth")
    crop_length = amino_share * col_count
    block_i = crop_length // row_count
    quarter = amino_share // depth_count
    row_idx = lax.axis_index("row")
    col_idx = lax.axis_index("col")
    standardized_alignment, standardize_backprop = jax.vjp(
        standardize_channels, alignment_matrix.astype(jnp.float32)
    )
    normed = standardized_alignment.astype(jnp.bfloat16)
    panels = jnp.dot(normed, twin_linear_matrix, preferred_element_type=jnp.float32).astype(
        jnp.bfloat16
    )
    left_local = panels[..., :latent_features]
    right_local = panels[..., latent_features:]
    left_every = lax.all_gather(left_local, "col", axis=1, tiled=True)
    left_rows = lax.dynamic_slice_in_dim(left_every, row_idx * block_i, block_i, 1)
    left_seqs = lax.all_gather(left_rows, "depth", axis=0, tiled=True)
    right_seqs = lax.all_to_all(right_local, "depth", split_axis=1, concat_axis=0, tiled=True)
    seq_count = left_seqs.shape[0]
    summed = jnp.einsum(
        "sje,sic->jice", right_seqs, left_seqs, preferred_element_type=jnp.float32
    ).reshape(quarter, block_i, latent_features * latent_features)
    outer_mean = (summed / seq_count).astype(jnp.bfloat16)
    pair_cols = jnp.dot(outer_mean, final_matrix, preferred_element_type=jnp.float32) + final_offset
    contact_delta = jnp.transpose(pair_cols, (1, 0, 2)).astype(jnp.bfloat16)
    adjoint_kronecker = (
        jnp.einsum(
            "gtz,vz->gtv", adjoint_incoming, final_matrix, preferred_element_type=jnp.float32
        )
        / seq_count
    ).astype(jnp.bfloat16)
    grad_four = adjoint_kronecker.reshape(block_i, quarter, latent_features, latent_features)
    adjoint_leftside = jnp.einsum(
        "ijce,sje->sic", grad_four, right_seqs, preferred_element_type=jnp.float32
    )
    grad_right = jnp.einsum(
        "ijce,sic->sje", grad_four, left_seqs, preferred_element_type=jnp.float32
    )
    w_local = jnp.einsum(
        "jif,ijo->fo", outer_mean, adjoint_incoming, preferred_element_type=jnp.float32
    )
    b_local = jnp.sum(adjoint_incoming.astype(jnp.float32), axis=(0, 1))
    weight_gradient, bias_gradient = in_one((w_local, b_local), ("row", "col", "depth"))
    left_back, right_back = (
        lax.all_to_all(adjoint_leftside, "depth", split_axis=0, concat_axis=1, tiled=True),
        lax.all_to_all(grad_right, "depth", split_axis=0, concat_axis=1, tiled=True),
    )
    left_back = jnp.sum(
        left_back.reshape(alignment_share, depth_count, block_i, latent_features), axis=1
    )
    left_summed = lax.psum(left_back, "col")
    owner_row = col_idx * amino_share // block_i
    left_full = broadcast(left_summed.astype(jnp.bfloat16), "row", owner_row).astype(
        left_summed.dtype
    )
    right_full = of_everyone(right_back, "row")
    both_grads = jnp.concatenate([left_full, right_full], axis=-1)
    grad_panels = both_grads.astype(jnp.bfloat16)
    standardized_adjoint = jnp.einsum(
        "slk,mk->slm", grad_panels, twin_linear_matrix, preferred_element_type=jnp.float32
    )
    alignment_adjoint = standardize_backprop(standardized_adjoint)[0]
    return (
        contact_delta,
        alignment_adjoint,
        weight_gradient / crop_length,
        bias_gradient / crop_length,
    )


def solution(mesh):
    in_specs = (P("depth", "col", None), P(), P(), P(), P("row", ("col", "depth"), None))
    out_specs = (P("row", ("col", "depth"), None), P("depth", "col", None), P(), P())
    return jax.shard_map(body, mesh=mesh, in_specs=in_specs, out_specs=out_specs, check_vma=False)
```

profile of v0, /device:TPU:1, one launch (start us, length us, event | category | flops | bytes accessed | tf_op | source)
XLA Modules:
  0.0 472.1 jit_solution(5661845479301086679)
XLA Ops:
  8.1 2.1 convert_reduce_fusion
  10.2 2.4 fusion.8
  12.7 1.3 fusion.16
  14.1 2.0 copy.31
  16.2 1.2 copy.33
  17.4 1.4 reshape.73
  18.8 5.0 %all-to-all-start = ((bf16[4,2,12288]{2,1,0:T(2,128)(2,1)}), bf16[4,2,12288]{2,1,0:T(2,128)(2,1)S(1)}, u32[]{:S(2)}, u32[]{:S(2)}) async-start(bf16[4,2,12288]{2,1,0:T(2,128)(2,1)} %reshape.73), calls=%async_computation | async-start | bytes 393216 | tf_op jit(solution)/shard_map/all_to_all | solution.py:61
  23.8 3.5 multiply_convert_fusion.1
  27.3 8.5 %copy.39 = bf16[96,24,1024]{0,2,1:T(8,128)(2,1)} copy(bf16[96,24,1024]{2,1,0:T(8,128)(2,1)} %multiply_convert_fusion.1) | data formatting | bytes 9437184 | tf_op jit(solution)/shard_map/convert_element_type | solution.py:74
  35.8 0.4 reshape.74
  36.2 0.6 copy.56
  36.8 1.1 reshape.66
  37.9 5.1 %convolution_bitcast_fusion.1 = f32[128,96,32]{0,1,2:T(8,128)S(1)} fusion(bf16[96,24,32,32]{0,3,2,1:T(8,128)(2,1)} %bitcast.63, bf16[128,24,32,1]{0,2,1,3:T(8,128)(2,1)} %reshape.66), kind=kOutput, calls=%fused_computation.20 | convolution fusion | flops 603979776 | bytes 6488064 | tf_op jit(solution)/shard_map/ijce,sje->sic/dot_general | solution.py:76
  43.0 1.9 copy.41
  44.9 4.8 %all-to-all-start.1 = ((f32[128,96,32]{1,2,0:T(8,128)}), f32[128,96,32]{1,2,0:T(8,128)}, u32[]{:S(2)}, u32[]{:S(2)}) async-start(f32[128,96,32]{1,2,0:T(8,128)} %copy.41), calls=%async_computation.1 | async-start | bytes 4194304 | tf_op jit(solution)/shard_map/all_to_all | solution.py:88
  50.0 24.5 %all-to-all-done.1 = f32[128,96,32]{1,2,0:T(8,128)} async-done(((f32[128,96,32]{1,2,0:T(8,128)}), f32[128,96,32]{1,2,0:T(8,128)}, u32[]{:S(2)}, u32[]{:S(2)}) %all-to-all-start.1) | async-done | bytes 1572896 | tf_op jit(solution)/shard_map/all_to_all | solution.py:88
  74.6 2.7 reduce_sum.82
  77.3 13.4 %all-gather.4.cloned.1.call-done = bf16[32,768,32]{2,0,1:T(8,128)(2,1)} async-done(((bf16[32,96,32]{2,0,1:T(8,128)(2,1)}), bf16[32,768,32]{2,0,1:T(8,128)(2,1)}) %all-gather.4.cloned.1.call-update) | async-done | bytes 1572880 | tf_op jit(solution)/shard_map/all_gather | solution.py:58
  90.6 1.2 constant_dynamic-slice_fusion
  91.8 0.8 copy.32
  92.6 13.8 %all_gather.13 = bf16[128,96,32]{1,2,0:T(8,128)(2,1)S(1)} all-gather(bf16[32,96,32]{1,2,0:T(8,128)(2,1)S(1)} %copy.32), channel_id=1, replica_groups=mesh['row'=8,'col'=8,'depth'=4] {'depth'}, dimensions={0}, use_global_device_ids=true | all-gather | bytes 983040 | tf_op jit(solution)/shard_map/all_gather | solution.py:60
  106.4 5.0 %convolution_bitcast_fusion.2 = f32[128,24,32]{0,2,1:T(8,128)S(1)} fusion(bf16[96,24,32,32]{0,3,2,1:T(8,128)(2,1)} %bitcast.64, bf16[128,96,32]{1,2,0:T(8,128)(2,1)S(1)} %all_gather.13), kind=kOutput, calls=%fused_computation.25 | convolution fusion | flops 603979776 | bytes 5898240 | tf_op jit(solution)/shard_map/ijce,sic->sje/dot_general | solution.py:79
  111.4 2.4 copy.48
  113.9 1.6 copy.43
  115.5 2.8 reshape.75
  118.3 3.5 all-to-all-start.2
  121.8 9.1 %fusion = bf16[24,96,32,32]{3,2,0,1:T(8,128)(2,1)} fusion(bf16[128,96,32,1]{0,2,3,1:T(8,128)(2,1)S(1)} %copy.48, bf16[128,24,32,1]{0,2,1,3:T(8,128)(2,1)S(1)} %copy-done.7), kind=kOutput, calls=%fused_computation.1 | convolution fusion | flops 608698368 | bytes 5701632 | tf_op jit(solution)/shard_map/sje,sic->jice/dot_general | solution.py:63
  130.9 20.1 %copy.37 = bf16[24,96,32,32]{1,3,2,0:T(8,128)(2,1)} copy(bf16[24,96,32,32]{3,2,0,1:T(8,128)(2,1)} %fusion) | data formatting | bytes 9437184 | tf_op jit(solution)/shard_map/convert_element_type | solution.py:66
  151.0 0.5 broadcast.58
  151.5 2.5 reduce.2
  154.0 1.5 reshape.76
  155.5 1.8 copy.44
  157.4 2.4 all_to_all.47
  159.8 2.5 broadcast_in_dim.4
  162.3 4.7 all-to-all-start.3
  167.3 4.3 convolution_bitcast_fusion
  171.6 0.8 pad_maximum_fusion
  172.6 66.0 %all-reduce.4 = bf16[32,96,32]{1,2,0:T(8,128)(2,1)} all-reduce(f32[32,96,32]{1,2,0:T(8,128)S(1)} %copy-done.6), channel_id=1, replica_groups=mesh['row'=8,'col'=8,'depth'=4] {'col'}, use_global_device_ids=true, to_apply=%region_3.0 | all-reduce | flops 98304 | bytes 589824 | tf_op jit(solution)/shard_map/psum | solution.py:94
  238.7 4.6 fusion.19
  243.3 1.0 copy.47
  244.3 205.4 %all-reduce.3.cloned.1.call-done = f32[131200]{0:T(1024)} async-done(((f32[131200]{0:T(1024)}), f32[131200]{0:T(1024)}) %all-reduce.3.cloned.1.call-update) | async-done | bytes 524816 | tf_op jit(solution)/shard_map/psum | solution.py:11
  449.8 1.2 slice_multiply_fusion.1
  450.9 1.9 fusion.23
  452.8 1.0 dynamic-slice_bitcast_fusion
  453.8 2.8 reduce_sum.83
  456.6 3.2 multiply_reduce_fusion
  459.9 1.6 fusion.5
  461.5 3.2 fusion.7
  (36 shorter events, 0.9 us)
Async XLA Ops:
  8.0 15.8 %copy-start = (bf16[1024,128]{1,0:T(8,128)(2,1)S(1)}, bf16[1024,128]{1,0:T(8,128)(2,1)}, u32[]{:S(2)}) copy-start(bf16[1024,128]{1,0:T(8,128)(2,1)} %param.7) | copy-start | bytes 786436
  8.0 4.7 copy-start.1
  8.0 4.7 copy-start.8
  8.0 82.6 %all-gather.4.cloned.1.call-start = ((), (), s32[]{:S(2)}) async-start(), calls=%async_computation.4 | async-start | bytes 7077888 | tf_op jit(solution)/shard_map/all_gather | solution.py:58
  14.1 9.8 %copy-start.3 = (bf16[96,24,128]{2,1,0:T(8,128)(2,1)S(1)}, bf16[96,24,128]{2,1,0:T(8,128)(2,1)}, u32[]{:S(2)}) copy-start(bf16[96,24,128]{2,1,0:T(8,128)(2,1)} %param.9) | copy-start | bytes 1769476
  18.8 17.0 %all-to-all-start = ((bf16[4,2,12288]{2,1,0:T(2,128)(2,1)}), bf16[4,2,12288]{2,1,0:T(2,128)(2,1)S(1)}, u32[]{:S(2)}, u32[]{:S(2)}) async-start(bf16[4,2,12288]{2,1,0:T(2,128)(2,1)} %reshape.73), calls=%async_computation | async-start | bytes 393216 | tf_op jit(solution)/shard_map/all_to_all | solution.py:61
  44.9 4.8 %copy-start.4 = (bf16[96,24,128]{2,1,0:T(8,128)(2,1)S(1)}, bf16[96,24,128]{2,1,0:T(8,128)(2,1)}, u32[]{:S(2)}) copy-start(bf16[96,24,128]{2,1,0:T(8,128)(2,1)} %param.9) | copy-start | bytes 1769476
  44.9 29.7 %all-to-all-start.1 = ((f32[128,96,32]{1,2,0:T(8,128)}), f32[128,96,32]{1,2,0:T(8,128)}, u32[]{:S(2)}, u32[]{:S(2)}) async-start(f32[128,96,32]{1,2,0:T(8,128)} %copy.41), calls=%async_computation.1 | async-start | bytes 4194304 | tf_op jit(solution)/shard_map/all_to_all | solution.py:88
  106.4 5.0 %copy-start.2 = (bf16[128,96,32]{1,2,0:T(8,128)(2,1)}, bf16[128,96,32]{1,2,0:T(8,128)(2,1)S(1)}, u32[]{:S(2)}) copy-start(bf16[128,96,32]{1,2,0:T(8,128)(2,1)S(1)} %all_gather.13) | copy-start | bytes 2359300
  111.4 10.4 %copy-start.7 = (bf16[128,24,32,1]{0,2,1,3:T(8,128)(2,1)S(1)}, bf16[128,24,32,1]{0,2,1,3:T(8,128)(2,1)}, u32[]{:S(2)}) copy-start(bf16[128,24,32,1]{0,2,1,3:T(8,128)(2,1)} %reshape.66) | copy-start | bytes 589828
  118.3 32.7 %all-to-all-start.2 = ((f32[4,1,24576]{2,1,0:T(1,128)}), f32[4,1,24576]{2,1,0:T(1,128)S(1)}, u32[]{:S(2)}, u32[]{:S(2)}) async-start(f32[4,1,24576]{2,1,0:T(1,128)} %reshape.75), calls=%async_computation.2 | async-start | bytes 786432 | tf_op jit(solution)/shard_map/all_to_all | solution.py:89
  162.3 5.0 %copy-start.5 = (bf16[96,24,128]{2,1,0:T(8,128)(2,1)S(1)}, bf16[96,24,128]{2,1,0:T(8,128)(2,1)}, u32[]{:S(2)}) copy-start(bf16[96,24,128]{2,1,0:T(8,128)(2,1)} %param.9) | copy-start | bytes 1769476
  162.3 291.5 %all-to-all-start.3 = ((f32[8,32,96,32]{2,3,1,0:T(8,128)}), f32[8,32,96,32]{2,3,1,0:T(8,128)}, u32[]{:S(2)}, u32[]{:S(2)}) async-start(f32[8,32,96,32]{2,3,1,0:T(8,128)} %broadcast_in_dim.4), calls=%async_computation.3 | async-start | bytes 8388608 | tf_op jit(solution)/shard_map/all_to_all | solution.py:24
  167.0 282.8 %all-reduce.3.cloned.1.call-start = ((), (), s32[]{:S(2)}) async-start(), calls=%async_computation.5 | async-start | bytes 1056768 | tf_op jit(solution)/shard_map/psum | solution.py:11
  167.3 5.3 %copy-start.6 = (f32[32,96,32]{1,2,0:T(8,128)S(1)}, f32[32,96,32]{1,2,0:T(8,128)}, u32[]{:S(2)}) copy-start(f32[32,96,32]{1,2,0:T(8,128)} %reduce_sum.82) | copy-start | bytes 1179652
  167.3 71.4 %copy-start.9 = (f32[128]{0:T(128)S(1)}, f32[128]{0:T(128)}, u32[]{:S(2)}) copy-start(f32[128]{0:T(128)} %param.8) | copy-start | bytes 1540
  172.5 280.3 %all-gather.6.cloned.1.call-start = ((), (), s32[]{:S(2)}) async-start(), calls=%async_computation.6 | async-start | bytes 2359296 | tf_op jit(solution)/shard_map/all_gather | solution.py:19
Sparse Core Ops, SparseCore 0:
  16.3 74.2 all-gather.3
  173.9 275.8 all-reduce.2
Sparse Core Ops, SparseCore 1:
  238.7 60.2 all-gather.5
where the time goes:
time: 474 us; the launch traced here: 472 us
  waiting for transfers between devices  243 us (51%)
  blocking collectives  79.8 us (17%)
  local copies, waits for them, and re-layouts  57 us (12%)
  matrix products  36.2 us (8%)
  other arithmetic  21.6 us (5%)
  starting transfers between devices  18.3 us (4%)
  between operations  15.8 us (3%)
    psum x1, waiting for transfers between devices, in_one(): running = lax.psum(vector, axis)  205 us
    psum x1, blocking collectives, body(): left_summed = lax.psum(left_back, 'col')  66 us
    all_to_all x1, waiting for transfers between devices, body(): lax.all_to_all(adjoint_leftside, 'depth', split_axis=0, concat_axis=1, ti...  24.5 us
    convert_element_type x1, local copies, waits for them, and re-layouts, body(): outer_mean = (summed / seq_count).astype(jnp.bfloat16)  20.1 us
    all_gather x1, blocking collectives, body(): left_seqs = lax.all_gather(left_rows, 'depth', axis=0, tiled=True)  13.8 us
    all_gather x1, waiting for transfers between devices, body(): left_every = lax.all_gather(left_local, 'col', axis=1, tiled=True)  13.4 us
  transfers between devices with their start and end apart: 7, of which 3 were waited for; matrix products, arithmetic and copies ran while one was open for 15% of the time, Pallas kernels for 0%

commit v1 on v0

--- a/solution.py
+++ b/solution.py
@@ -1,9 +1,17 @@
+import functools
 import jax
 import jax.numpy as jnp
 from jax import lax
 from jax.sharding import PartitionSpec as P
 
 epsilon = 1e-05
+
+
+def push_the_sheets(original, axis_name):
+    return jax.lax.all_gather(original, axis_name).sum(axis=0)
+
+
+_resolve_stocks = functools.partial(push_the_sheets, axis_name="col")
 
 
 def in_one(arrays, axis):
@@ -91,7 +99,7 @@
     left_back = jnp.sum(
         left_back.reshape(alignment_share, depth_count, block_i, latent_features), axis=1
     )
-    left_summed = lax.psum(left_back, "col")
+    left_summed = _resolve_stocks(left_back)
     owner_row = col_idx * amino_share // block_i
     left_full = broadcast(left_summed.astype(jnp.bfloat16), "row", owner_row).astype(
         left_summed.dtype

time: 474 us -> 498 us (1.051)
  waiting for transfers between devices: 243 us -> 307 us
  blocking collectives: 79.8 us -> 43 us
    psum x1 -> x0, blocking collectives: 66 us -> none  [body(): left_summed = lax.psum(left_back, 'col')]
    all_gather x1, waiting for transfers between devices: 0.01 us -> 47 us  [broadcast(): lax.all_gather(shard, axis)]
    psum x1, waiting for transfers between devices: 205 us -> 243 us  [in_one(): running = lax.psum(vector, axis)]
    all_to_all x0 -> x1, blocking collectives: none -> 29.1 us  [body(): lax.all_to_all(adjoint_leftside, 'depth', split_axis=0, concat_axis=1, ti...]
    all_to_all x1 -> x0, waiting for transfers between devices: 24.5 us -> none  [body(): lax.all_to_all(adjoint_leftside, 'depth', split_axis=0, concat_axis=1, ti...]
  transfers between devices with their start and end apart: 7 -> 7, of which waited for: 3 -> 4; matrix products, arithmetic and copies ran while one was open for 15% -> 20% of each run, Pallas kernels for 0% -> 0%
where the time goes in v1:
time: 498 us; the launch traced here: 497 us
  waiting for transfers between devices  307 us (62%)
  local copies, waits for them, and re-layouts  57.8 us (12%)
  blocking collectives  43 us (9%)
  matrix products  36.5 us (7%)
  other arithmetic  25.4 us (5%)
  between operations  14 us (3%)
  starting transfers between devices  13.5 us (3%)
    psum x1, waiting for transfers between devices, in_one(): running = lax.psum(vector, axis)  243 us
    all_gather x1, waiting for transfers between devices, broadcast(): lax.all_gather(shard, axis)  47 us
    all_to_all x1, blocking collectives, body(): lax.all_to_all(adjoint_leftside, 'depth', split_axis=0, concat_axis=1, ti...  29.1 us
    convert_element_type x1, local copies, waits for them, and re-layouts, body(): outer_mean = (summed / seq_count).astype(jnp.bfloat16)  20.2 us
    all_gather x1, waiting for transfers between devices, body(): left_every = lax.all_gather(left_local, 'col', axis=1, tiled=True)  13.9 us
    all_gather x1, blocking collectives, body(): left_seqs = lax.all_gather(left_rows, 'depth', axis=0, tiled=True)  13.9 us
  transfers between devices with their start and end apart: 7, of which 4 were waited for; matrix products, arithmetic and copies ran while one was open for 20% of the time, Pallas kernels for 0%

profile of v1, /device:TPU:1, one launch (start us, length us, event | category | flops | bytes accessed | tf_op | source)
XLA Modules:
  0.0 496.8 jit_solution(4450139544239095690)
XLA Ops:
  7.2 2.1 convert_reduce_fusion
  9.4 2.4 fusion.8
  11.9 1.3 fusion.16
  13.3 2.0 copy.31
  15.3 1.2 copy.33
  16.6 1.4 reshape.82
  18.0 5.0 %all-to-all-start = ((bf16[4,2,12288]{2,1,0:T(2,128)(2,1)}), bf16[4,2,12288]{2,1,0:T(2,128)(2,1)S(1)}, u32[]{:S(2)}, u32[]{:S(2)}) async-start(bf16[4,2,12288]{2,1,0:T(2,128)(2,1)} %reshape.82), calls=%async_computation | async-start | bytes 393216 | tf_op jit(solution)/shard_map/all_to_all | solution.py:69
  23.0 3.5 multiply_convert_fusion.1
  26.5 8.5 %copy.39 = bf16[96,24,1024]{0,2,1:T(8,128)(2,1)} copy(bf16[96,24,1024]{2,1,0:T(8,128)(2,1)} %multiply_convert_fusion.1) | data formatting | bytes 9437184 | tf_op jit(solution)/shard_map/convert_element_type | solution.py:82
  36.0 1.1 reshape.75
  37.1 5.1 %convolution_bitcast_fusion.1 = f32[128,96,32]{0,1,2:T(8,128)S(1)} fusion(bf16[96,24,32,32]{0,3,2,1:T(8,128)(2,1)} %bitcast.64, bf16[128,24,32,1]{0,2,1,3:T(8,128)(2,1)} %reshape.75), kind=kOutput, calls=%fused_computation.20 | convolution fusion | flops 603979776 | bytes 6488064 | tf_op jit(solution)/shard_map/ijce,sje->sic/dot_general | solution.py:84
  42.2 1.9 copy.41
  44.1 29.1 %all_to_all.53 = f32[128,96,32]{1,2,0:T(8,128)} all-to-all(f32[128,96,32]{1,2,0:T(8,128)} %copy.41), channel_id=1, replica_groups=mesh['row'=8,'col'=8,'depth'=4] {'depth'}, dimensions={0} | all-to-all | bytes 3145728 | tf_op jit(solution)/shard_map/all_to_all | solution.py:96
  73.2 2.7 reduce_sum.91
  75.9 13.9 %all-gather.6.cloned.1.call-done = bf16[32,768,32]{2,0,1:T(8,128)(2,1)} async-done(((bf16[32,96,32]{2,0,1:T(8,128)(2,1)}), bf16[32,768,32]{2,0,1:T(8,128)(2,1)}) %all-gather.6.cloned.1.call-update) | async-done | bytes 1572880 | tf_op jit(solution)/shard_map/all_gather | solution.py:66
  89.8 1.2 constant_dynamic-slice_fusion
  91.0 0.8 copy.32
  91.8 13.9 %all_gather.17 = bf16[128,96,32]{1,2,0:T(8,128)(2,1)S(1)} all-gather(bf16[32,96,32]{1,2,0:T(8,128)(2,1)S(1)} %copy.32), channel_id=1, replica_groups=mesh['row'=8,'col'=8,'depth'=4] {'depth'}, dimensions={0}, use_global_device_ids=true | all-gather | bytes 983040 | tf_op jit(solution)/shard_map/all_gather | solution.py:68
  105.8 1.0 copy-done.2
  106.7 5.3 %convolution_bitcast_fusion.2 = f32[128,24,32]{0,2,1:T(8,128)} fusion(bf16[96,24,32,32]{0,3,2,1:T(8,128)(2,1)} %bitcast.65, bf16[128,96,32]{1,2,0:T(8,128)(2,1)S(1)} %all_gather.17), kind=kOutput, calls=%fused_computation.25 | convolution fusion | flops 603979776 | bytes 5898240 | tf_op jit(solution)/shard_map/ijce,sic->sje/dot_general | solution.py:87
  112.1 1.5 copy.43
  113.6 1.4 reshape.84
  115.0 3.5 all-to-all-start.2
  118.5 1.4 convert_reduce_fusion.1
  119.9 2.4 copy.48
  122.3 2.6 all-to-all-done.2
  125.4 1.8 reduce.2
  127.2 1.7 reshape.85
  128.9 2.9 copy.44
  131.7 2.4 all_to_all.47
  134.1 2.6 broadcast_in_dim.4
  136.7 4.7 all-to-all-start.3
  141.7 9.1 %fusion = bf16[24,96,32,32]{3,2,0,1:T(8,128)(2,1)} fusion(bf16[128,96,32,1]{0,2,3,1:T(8,128)(2,1)S(1)} %copy.48, bf16[128,24,32,1]{0,2,1,3:T(8,128)(2,1)S(1)} %copy-done.5), kind=kOutput, calls=%fused_computation.1 | convolution fusion | flops 608698368 | bytes 5701632 | tf_op jit(solution)/shard_map/sje,sic->jice/dot_general | solution.py:71
  150.8 20.2 %copy.37 = bf16[24,96,32,32]{1,3,2,0:T(8,128)(2,1)} copy(bf16[24,96,32,32]{3,2,0,1:T(8,128)(2,1)} %fusion) | data formatting | bytes 9437184 | tf_op jit(solution)/shard_map/convert_element_type | solution.py:74
  171.0 4.3 convolution_bitcast_fusion
  175.3 0.8 pad_maximum_fusion
  176.2 3.5 reduce_sum.92
  179.8 4.6 fusion.19
  184.4 1.0 copy.47
  185.4 242.9 %all-reduce.2.cloned.1.call-done = f32[131200]{0:T(1024)} async-done(((f32[131200]{0:T(1024)}), f32[131200]{0:T(1024)}) %all-reduce.2.cloned.1.call-update) | async-done | bytes 524816 | tf_op jit(solution)/shard_map/psum | solution.py:19
  428.4 1.2 slice_multiply_fusion.1
  429.6 1.9 fusion.23
  431.4 2.8 reduce_sum.93
  434.2 47.0 %all-gather.10.cloned.1.call-done = bf16[256,96,32]{1,2,0:T(8,128)(2,1)} async-done(((bf16[32,96,32]{1,2,0:T(8,128)(2,1)}), bf16[256,96,32]{1,2,0:T(8,128)(2,1)}) %all-gather.10.cloned.1.call-update) | async-done | bytes 1572880 | tf_op jit(solution)/shard_map/all_gather | solution.py:27
  481.3 1.0 dynamic-slice_bitcast_fusion
  482.2 3.2 multiply_reduce_fusion
  485.5 1.6 fusion.5
  487.1 3.2 fusion.7
  (34 shorter events, 2.0 us)
Async XLA Ops:
  7.2 15.8 %copy-start = (bf16[1024,128]{1,0:T(8,128)(2,1)S(1)}, bf16[1024,128]{1,0:T(8,128)(2,1)}, u32[]{:S(2)}) copy-start(bf16[1024,128]{1,0:T(8,128)(2,1)} %param.7) | copy-start | bytes 786436
  7.2 4.7 copy-start.1
  7.2 4.7 copy-start.6
  7.2 82.6 %all-gather.6.cloned.1.call-start = ((), (), s32[]{:S(2)}) async-start(), calls=%async_computation.4 | async-start | bytes 7077888 | tf_op jit(solution)/shard_map/all_gather | solution.py:66
  13.2 9.8 %copy-start.3 = (bf16[96,24,128]{2,1,0:T(8,128)(2,1)S(1)}, bf16[96,24,128]{2,1,0:T(8,128)(2,1)}, u32[]{:S(2)}) copy-start(bf16[96,24,128]{2,1,0:T(8,128)(2,1)} %param.9) | copy-start | bytes 1769476
  18.0 17.0 %all-to-all-start = ((bf16[4,2,12288]{2,1,0:T(2,128)(2,1)}), bf16[4,2,12288]{2,1,0:T(2,128)(2,1)S(1)}, u32[]{:S(2)}, u32[]{:S(2)}) async-start(bf16[4,2,12288]{2,1,0:T(2,128)(2,1)} %reshape.82), calls=%async_computation | async-start | bytes 393216 | tf_op jit(solution)/shard_map/all_to_all | solution.py:69
  23.0 153.2 %all-gather.8.cloned.1.call-start = ((), (), s32[]{:S(2)}) async-start(), calls=%async_computation.6 | async-start | bytes 4718592 | tf_op jit(solution)/shard_map/all_gather | solution.py:11
  105.8 1.0 copy-start.2
  115.0 9.8 %all-to-all-start.2 = ((f32[4,1,24576]{2,1,0:T(1,128)}), f32[4,1,24576]{2,1,0:T(1,128)S(1)}, u32[]{:S(2)}, u32[]{:S(2)}) async-start(f32[4,1,24576]{2,1,0:T(1,128)} %reshape.84), calls=%async_computation.2 | async-start | bytes 786432 | tf_op jit(solution)/shard_map/all_to_all | solution.py:97
  136.7 5.0 %copy-start.5 = (bf16[128,24,32,1]{0,2,1,3:T(8,128)(2,1)S(1)}, bf16[128,24,32,1]{0,2,1,3:T(8,128)(2,1)}, u32[]{:S(2)}) copy-start(bf16[128,24,32,1]{0,2,1,3:T(8,128)(2,1)} %reshape.75) | copy-start | bytes 589828
  136.7 294.7 %all-to-all-start.3 = ((f32[8,32,96,32]{2,3,1,0:T(8,128)}), f32[8,32,96,32]{2,3,1,0:T(8,128)}, u32[]{:S(2)}, u32[]{:S(2)}) async-start(f32[8,32,96,32]{2,3,1,0:T(8,128)} %broadcast_in_dim.4), calls=%async_computation.3 | async-start | bytes 8388608 | tf_op jit(solution)/shard_map/all_to_all | solution.py:32
  141.5 286.9 %all-reduce.2.cloned.1.call-start = ((), (), s32[]{:S(2)}) async-start(), calls=%async_computation.5 | async-start | bytes 1056768 | tf_op jit(solution)/shard_map/psum | solution.py:19
  150.8 20.2 %copy-start.4 = (bf16[96,24,128]{2,1,0:T(8,128)(2,1)S(1)}, bf16[96,24,128]{2,1,0:T(8,128)(2,1)}, u32[]{:S(2)}) copy-start(bf16[96,24,128]{2,1,0:T(8,128)(2,1)} %param.9) | copy-start | bytes 1769476
  175.3 4.5 copy-start.7
  176.1 305.1 %all-gather.10.cloned.1.call-start = ((), (), s32[]{:S(2)}) async-start(), calls=%async_computation.7 | async-start | bytes 2359296 | tf_op jit(solution)/shard_map/all_gather | solution.py:27
Sparse Core Ops, SparseCore 0:
  15.5 74.3 all-gather.5
  92.3 51.3 all-gather.7
  176.3 252.0 all-reduce.1
  430.0 51.2 all-gather.9
